TPU v7x, 512 devices: a whole 4x8x8 slice. The times are simulated.
512 devices in a mesh: learner: 32 (over x, y), tensor: 16 (over z, core).
Axes of the slice: x: 4, y: 8, z: 8, core: 2. Of those that a mesh axis runs over, the one named last changes fastest.
Arguments:
- blocks: bfloat16 [256, 128, 4096], P('learner', None, 'tensor'), may hold values from -60 to 60
- seg_ids: int32 [32, 1024], P('learner'), may hold values from 0 to 7, never falling along the last dimension, each value on 1 to 256 neighbouring positions
- dest: int32 [256], replicated, may hold values from 0 to 31, as said below
- slot: int32 [256], replicated, may hold values from 0 to 7, as said below
- norm_gain: bfloat16 [4096], P('tensor'), may hold values from 0.25 to 1.75
- w_query: bfloat16 [4096, 4096], P(None, 'tensor'), may hold values from -2 to 2
- w_keyval: bfloat16 [4096, 2048], P('learner'), may hold values from -2 to 2
Outputs:
- context: bfloat16 [32768, 4096], P('learner', 'tensor')
Inputs may be any that keep to these rules, and one draw needn't show every extreme that they name: `dest`: each learner receives exactly 8 blocks; at most 1 of the blocks of one learner go to any one learner, and in every draw some learner sends exactly 1 block to one learner. `slot`: the blocks that one learner receives take the positions 0 to 7 of its packed row, one each.
All inputs are finite; a program needn't handle non-finite values.
Results may differ from a plain program's by a relative error of at most 0.012.
The roundings to bfloat16 on the way count: a program that leaves them out, or rounds other values in their place, can miss the bound.
Values may be sent and summed in bfloat16 or wider, within the bound.
A program may use at most 64 MiB of HBM per device.

v0:
```python
import math

import jax
import jax.numpy as jnp
from jax import lax
from jax.sharding import PartitionSpec as P

D = 4096
HEADS = 32
KV_HEADS = 8
HD = 128


def copy_for_each(x, axis):
    count = lax.axis_size(axis)
    return lax.all_to_all(jnp.broadcast_to(x[None], (count, *x.shape)), axis, 0, 0, tiled=True)


def joined_along(tiles, dim):
    tiles = jnp.moveaxis(tiles, 0, dim)
    shape = tiles.shape
    return tiles.reshape(*shape[:dim], shape[dim] * shape[dim + 1], *shape[dim + 2 :])


def gather_directly(x, axis, dim):
    tiles = copy_for_each(x, axis)
    return joined_along(tiles, dim)


def in_one_piece(arrays, axis, dim, along):
    both = jnp.concatenate(arrays, axis=along)
    out, at, finished = (lax.all_gather(both, axis, axis=dim, tiled=True), 0, [])
    for a in arrays:
        finished.append(lax.slice_in_dim(out, at, at + a.shape[along], axis=along))
        at += a.shape[along]
    return tuple(finished)


def on_device(blocks, seg_ids, dest, slot, norm_gain, w_query, w_keyval):
    learners = lax.axis_size("learner")
    own_index = lax.axis_index("learner")
    blk_dev, block_len, features = blocks.shape
    capacity = (blk_dev + learners - 1) // learners
    targets = dest.reshape(learners, blk_dev)
    places = slot.reshape(learners, blk_dev)
    block_ids = jnp.arange(blk_dev, dtype=jnp.int32)
    earlier = block_ids[None, :] < block_ids[:, None]
    same_target = targets[:, :, None] == targets[:, None, :]
    ranks = jnp.sum(jnp.where(same_target & earlier[None], 1, 0), axis=2).astype(jnp.int32)
    own_targets = lax.dynamic_index_in_dim(targets, own_index, 0, keepdims=False)
    own_ranks = lax.dynamic_index_in_dim(ranks, own_index, 0, keepdims=False)
    send_slots = own_targets * capacity + own_ranks
    slot_range = jnp.arange(learners * capacity, dtype=jnp.int32)
    send_table = (send_slots[None, :] == slot_range[:, None]).astype(jnp.bfloat16)
    outgoing = jnp.dot(send_table, blocks.reshape(blk_dev, -1), preferred_element_type=jnp.float32)
    outgoing = outgoing.astype(jnp.bfloat16).reshape(learners * capacity, block_len, features)
    incoming = lax.all_to_all(outgoing, "learner", split_axis=0, concat_axis=0, tiled=True)
    arrive = (targets == own_index).reshape(-1)
    source_slots = (jnp.arange(learners, dtype=jnp.int32)[:, None] * capacity + ranks).reshape(-1)
    place_hot = ((places.reshape(-1)[:, None] == block_ids[None, :]) & arrive[:, None]).astype(
        jnp.float32
    )
    source_hot = (source_slots[:, None] == slot_range[None, :]).astype(jnp.float32)
    receive_table = jnp.dot(place_hot.T, source_hot).astype(jnp.bfloat16)
    local = jnp.dot(
        receive_table, incoming.reshape(learners * capacity, -1), preferred_element_type=jnp.float32
    )
    local = local.astype(jnp.bfloat16).reshape(blk_dev * block_len, features)
    heads_dev = w_query.shape[1] // HD
    per_group = HEADS // KV_HEADS
    groups_dev = max(1, heads_dev // per_group)
    first_group = lax.axis_index("tensor") * heads_dev // per_group
    kv_columns = lax.dynamic_slice_in_dim(w_keyval, first_group * 2 * HD, groups_dev * 2 * HD, 1)
    kv_weight = gather_directly(kv_columns, "learner", 0)
    whole_rows, gain_row = in_one_piece((local, norm_gain.reshape(1, -1)), "tensor", 1, 0)
    squares = jnp.einsum("rd,rd->r", whole_rows, whole_rows, preferred_element_type=jnp.float32)
    inverse_rms = lax.rsqrt(squares / D + 1e-05)
    normed = (
        whole_rows.astype(jnp.float32) * inverse_rms[:, None] * gain_row.astype(jnp.float32)
    ).astype(jnp.bfloat16)
    queries = jnp.dot(normed, w_query, preferred_element_type=jnp.float32).astype(jnp.bfloat16)
    keyval = jnp.dot(normed, kv_weight, preferred_element_type=jnp.float32).astype(jnp.bfloat16)
    row_count = queries.shape[0]
    paired = keyval.reshape(row_count, groups_dev, 2, HD)
    key_local = paired[:, :, 0, :]
    value_local = paired[:, :, 1, :]
    heads_per_group = heads_dev // groups_dev
    query_block = 512
    block_count = row_count // query_block
    query_parts = queries.reshape(block_count, query_block, groups_dev, heads_per_group, HD)
    starts = jnp.arange(block_count, dtype=jnp.int32) * query_block
    segment = seg_ids.reshape(-1)
    key_index = jnp.arange(row_count, dtype=jnp.int32)

    def attend(item):
        query_part, start = item
        scores = jnp.einsum(
            "qgpd,kgd->gpqk", query_part, key_local, preferred_element_type=jnp.float32
        ) / math.sqrt(HD)
        query_index = start + jnp.arange(query_block, dtype=jnp.int32)
        query_segment = lax.dynamic_slice_in_dim(segment, start, query_block, 0)
        allowed = (query_segment[:, None] == segment[None, :]) & (
            key_index[None, :] <= query_index[:, None]
        )
        masked = jnp.where(allowed[None, None], scores, -1e30)
        row_max = jnp.max(masked, axis=-1, keepdims=True)
        exponent = jnp.where(allowed[None, None], jnp.exp(masked - row_max), 0.0)
        probs = (exponent / jnp.sum(exponent, axis=-1, keepdims=True)).astype(jnp.bfloat16)
        context = jnp.einsum(
            "gpqk,kgd->qgpd", probs, value_local, preferred_element_type=jnp.float32
        )
        return context.astype(jnp.bfloat16).reshape(query_block, heads_dev * HD)

    result = lax.map(attend, (query_parts, starts))
    return result.reshape(row_count, heads_dev * HD)


def solution(mesh):
    return jax.shard_map(
        on_device,
        mesh=mesh,
        in_specs=(
            P("learner", None, "tensor"),
            P("learner", None),
            P(),
            P(),
            P("tensor"),
            P(None, "tensor"),
            P("learner", None),
        ),
        out_specs=P("learner", "tensor"),
        check_vma=False,
    )
```

profile of v0, /device:TPU:1, one launch (start us, length us, event | category | flops | bytes accessed | tf_op | source)
XLA Modules:
  0.0 196.3 jit_solution(14401464460937735717)
XLA Ops:
  6.5 0.9 eq.86
  7.5 1.3 copy.35
  9.9 1.8 copy.36
  11.7 10.7 %all-to-all-start = ((bf16[32,128,256]{2,1,0:T(8,128)(2,1)}), bf16[32,128,256]{2,1,0:T(8,128)(2,1)}, u32[]{:S(2)}, u32[]{:S(2)}) async-start(bf16[32,128,256]{2,1,0:T(8,128)(2,1)} %bitcast.86), calls=%async_computation | async-start | bytes 4194304 | tf_op jit(solution)/shard_map/all_to_all | solution.py:57
  22.7 48.6 %all-to-all-done = bf16[32,128,256]{2,1,0:T(8,128)(2,1)} async-done(((bf16[32,128,256]{2,1,0:T(8,128)(2,1)}), bf16[32,128,256]{2,1,0:T(8,128)(2,1)}, u32[]{:S(2)}, u32[]{:S(2)}) %all-to-all-start) | async-done | bytes 2097184 | tf_op jit(solution)/shard_map/all_to_all | solution.py:57
  71.3 4.1 %copy.37 = bf16[4,8,128,256]{3,1,2,0:T(8,128)(2,1)} copy(bf16[4,8,128,256]{3,2,1,0:T(8,128)(2,1)} %bitcast.31) | data formatting | bytes 4194304
  75.4 2.3 %convolution_convert_fusion.1 = bf16[8,32768]{1,0:T(8,128)(2,1)S(1)} fusion(bf16[32,32768]{1,0:T(8,128)(2,1)} %bitcast.87, s32[256]{0:T(256)S(1)} %add.54, s32[256]{0:T(256)S(1)} %copy-done.4, pred[256]{0:T(512)(128)(4,1)S(1)} %broadcast_compare_fusion), kind=kOutput, calls=%fused_computation.22 | convolution fusion | flops 17182976 | bytes 2623744 | tf_op jit(solution)/shard_map/dot_general | solution.py:65
  77.9 0.9 pad_maximum_fusion
  78.8 0.8 constant_dynamic-slice_fusion.1
  79.7 1.6 broadcast_in_dim.58
  81.2 7.3 %all-to-all-start.1 = ((bf16[32,128,256]{2,1,0:T(8,128)(2,1)}), bf16[32,128,256]{2,1,0:T(8,128)(2,1)}, u32[]{:S(2)}, u32[]{:S(2)}) async-start(bf16[32,128,256]{2,1,0:T(8,128)(2,1)} %broadcast_in_dim.58), calls=%async_computation.1 | async-start | bytes 4194304 | tf_op jit(solution)/shard_map/all_to_all | solution.py:16
  88.6 62.6 %all-gather.2.cloned.1.call-done = bf16[1025,4096]{1,0:T(8,128)(2,1)} async-done(((bf16[1025,256]{1,0:T(8,128)(2,1)}), bf16[1025,4096]{1,0:T(8,128)(2,1)}) %all-gather.2.cloned.1.call-update) | async-done | bytes 8396816 | tf_op jit(solution)/shard_map/all_gather | solution.py:32
  151.2 5.1 %fusion.18 = f32[1024]{0:T(1024)S(1)} fusion(bf16[1025,4096]{1,0:T(8,128)(2,1)} %all-gather.2.cloned.1.call-done), kind=kLoop, calls=%fused_computation.27 | loop fusion | flops 12581888 | bytes 8392704 | tf_op jit(solution)/shard_map/rd,rd->r/dot_general | solution.py:76
  156.2 0.9 slice_convert_fusion
  157.1 6.6 %fusion.26 = bf16[1024,256]{0,1:T(8,128)(2,1)S(1)} fusion(bf16[4096,256]{1,0:T(8,128)(2,1)} %bitcast.2, f32[4096]{0:T(1024)S(1)} %bitcast.98, f32[1024]{0:T(1024)S(1)} %add_rsqrt_fusion, bf16[1025,4096]{1,0:T(8,128)(2,1)} %all-gather.2.cloned.1.call-done), kind=kOutput, calls=%fused_computation.31 | convolution fusion | flops 2164523008 | bytes 11030528 | tf_op jit(solution)/shard_map/dot_general | solution.py:82
  163.7 0.8 slice_bitcast_fusion
  164.7 5.8 %fusion.23 = bf16[1024,256]{1,0:T(8,128)(2,1)S(1)} fusion(bf16[4096,256]{1,0:T(8,128)(2,1)S(1)} %copy-done, f32[4096]{0:T(1024)S(1)} %bitcast.99, f32[1024]{0:T(1024)S(1)} %add_rsqrt_fusion, bf16[1025,4096]{1,0:T(8,128)(2,1)} %all-gather.2.cloned.1.call-done), kind=kOutput, calls=%fused_computation.30 | convolution fusion | flops 2164523008 | bytes 11030528 | tf_op jit(solution)/shard_map/dot_general | solution.py:81
  170.6 18.9 %while.11 = (s32[]{:T(128)}, bf16[2,512,256]{2,1,0:T(8,128)(2,1)}, s32[2]{0:T(128)S(1)}, s32[1024]{0:T(1024)S(1)}, s32[1,1024]{1,0:T(1,128)S(1)}, /*index=5*/bf1...) while((s32[]{:T(128)}, bf16[2,512,256]{2,1,0:T(8,128)(2,1)}, ...), condition=%wide.region_4.5_spmd.clone, body=%wide.region_1.4_spmd.clone.sunk | while | flops 553253376 | bytes 18385604 | solution.py:114
  174.9 1.1 fusion.52
  176.0 1.5 fusion.53
  177.5 1.7 fusion.54
  184.3 1.1 fusion.52
  185.5 1.5 fusion.53
  186.9 1.7 fusion.54
  (47 shorter events, 7.9 us)
Async XLA Ops:
  6.5 158.1 %copy-start = (bf16[4096,256]{1,0:T(8,128)(2,1)S(1)}, bf16[4096,256]{1,0:T(8,128)(2,1)}, u32[]{:S(2)}) copy-start(bf16[4096,256]{1,0:T(8,128)(2,1)} %param.14) | copy-start | bytes 6291460
  9.8 12.8 %copy-start.5 = (bf16[256]{0:T(256)(128)(2,1)S(1)}, bf16[256]{0:T(256)(128)(2,1)}, u32[]{:S(2)}) copy-start(bf16[256]{0:T(256)(128)(2,1)} %param.13) | copy-start | bytes 1540
  9.8 12.8 %copy-start.3 = (s32[256]{0:T(256)S(1)}, s32[256]{0:T(256)}, u32[]{:S(2)}) copy-start(s32[256]{0:T(256)} %param.11) | copy-start | bytes 3076
  11.7 63.7 %copy-start.4 = (s32[256]{0:T(256)S(1)}, s32[256]{0:T(256)}, u32[]{:S(2)}) copy-start(s32[256]{0:T(256)} %param.12) | copy-start | bytes 3076
  11.7 59.7 %all-to-all-start = ((bf16[32,128,256]{2,1,0:T(8,128)(2,1)}), bf16[32,128,256]{2,1,0:T(8,128)(2,1)}, u32[]{:S(2)}, u32[]{:S(2)}) async-start(bf16[32,128,256]{2,1,0:T(8,128)(2,1)} %bitcast.86), calls=%async_computation | async-start | bytes 4194304 | tf_op jit(solution)/shard_map/all_to_all | solution.py:57
  22.4 128.7 %all-gather.2.cloned.1.call-start = ((), (), s32[]{:S(2)}) async-start(), calls=%async_computation.2 | async-start | bytes 8982528 | tf_op jit(solution)/shard_map/all_gather | solution.py:32
  81.2 75.9 %all-to-all-start.1 = ((bf16[32,128,256]{2,1,0:T(8,128)(2,1)}), bf16[32,128,256]{2,1,0:T(8,128)(2,1)}, u32[]{:S(2)}, u32[]{:S(2)}) async-start(bf16[32,128,256]{2,1,0:T(8,128)(2,1)} %broadcast_in_dim.58), calls=%async_computation.1 | async-start | bytes 4194304 | tf_op jit(solution)/shard_map/all_to_all | solution.py:16
  164.7 5.9 %copy-start.2 = (s32[1,1024]{1,0:T(1,128)S(1)}, s32[1,1024]{1,0:T(1,128)}, u32[]{:S(2)}) copy-start(s32[1,1024]{1,0:T(1,128)} %param.10) | copy-start | bytes 12292
  174.9 2.6 %copy-start.1 = (bf16[1024,1,128]{0,2,1:T(8,128)(2,1)S(1)}, bf16[1024,1,128]{0,2,1:T(8,128)(2,1)}, u32[]{:S(2)}) copy-start(bf16[1024,1,128]{0,2,1:T(8,128)(2,1)} %get-tuple-element.205) | copy-start | bytes 786436 | tf_op jit(solution)/shard_map/while
  184.3 2.6 %copy-start.1 = (bf16[1024,1,128]{0,2,1:T(8,128)(2,1)S(1)}, bf16[1024,1,128]{0,2,1:T(8,128)(2,1)}, u32[]{:S(2)}) copy-start(bf16[1024,1,128]{0,2,1:T(8,128)(2,1)} %get-tuple-element.205) | copy-start | bytes 786436 | tf_op jit(solution)/shard_map/while
Sparse Core Ops, SparseCore 0:
  78.9 72.1 all-gather.1
where the time goes:
time: 197 us; the launch traced here: 196 us
  waiting for transfers between devices  111 us (56%)
  matrix products  21 us (11%)
  starting transfers between devices  18.1 us (9%)
  local copies, waits for them, and re-layouts  15.7 us (8%)
  between operations  13.6 us (7%)
  other arithmetic  12.5 us (6%)
  loops' own time  4.2 us (2%)
    all_gather x1, waiting for transfers between devices, in_one_piece(): lax.all_gather(both, axis, axis=dim, tiled=True)  62.6 us
    all_to_all x1, waiting for transfers between devices, on_device(): lax.all_to_all(outgoing, 'learner', split_axis=0, concat_axis=0, tiled=True)  48.6 us
    all_to_all x1, starting transfers between devices, on_device(): lax.all_to_all(outgoing, 'learner', split_axis=0, concat_axis=0, tiled=True)  10.7 us
    unnamed x14, local copies, waits for them, and re-layouts  7.42 us
    all_to_all x1, starting transfers between devices, copy_for_each(): lax.all_to_all(jnp.broadcast_to(x[None], (count, *x.shape)), axis, 0, 0,...  7.31 us
    dot_general x1, matrix products, on_device(): jnp.dot(normed, kv_weight, preferred_element_type=jnp.float32)  6.63 us
    dot_general x1, matrix products, on_device(): jnp.dot(normed, w_query, preferred_element_type=jnp.float32)  5.77 us
    dot_general x1, other arithmetic, on_device(): jnp.einsum('rd,rd->r', whole_rows, whole_rows, preferred_element_type=jnp...  5.07 us
  transfers between devices with their start and end apart: 3, of which 2 were waited for; matrix products, arithmetic and copies ran while one was open for 4% of the time, Pallas kernels for 0%

commit v1 on v0

v1 whole, which is shorter than its diff:
```python
import functools
import math

import jax
import jax.numpy as jnp
from jax import lax
from jax.experimental import pallas as pl
from jax.experimental.pallas import tpu as pltpu
from jax.sharding import PartitionSpec as P

D = 4096
HEADS = 32
KV_HEADS = 8
HD = 128
MESH = pl.DeviceIdType.MESH
F32 = jnp.float32
BF16 = jnp.bfloat16
TILES = 130
HALF = 65


def comm_kernel(
    inv, blocks, gain, wkv, xall, wout,
    gathered, sorted_, landed,
    local_sem, send_a, recv_a, send_b, recv_b,
    send_z, recv_z, send_d, recv_d,
    send_w, recv_wy, recv_wx, recv_wd,
):
    l = lax.axis_index("learner")
    t = lax.axis_index("tensor")
    x, y = lax.div(l, 8), lax.rem(l, 8)
    z, c = lax.div(t, 2), lax.rem(t, 2)
    other = z * 2 + (1 - c)

    def plane(j):
        return (j, t)

    def at_offset(i):
        return lax.rem(x + lax.div(i, 8), 4) * 8 + lax.rem(y + lax.rem(i, 8), 8)

    def peer(i, f):
        return lax.rem(x + lax.div(i, 4), 4) * 8 + lax.rem(lax.div(y, 2) + lax.rem(i, 4), 4) * 2 + f

    def place(j):
        return lax.div(j, 8) * 4 + lax.div(lax.rem(j, 8), 2)

    own_f = lax.rem(y, 2)
    own_place = place(l)

    barrier = pltpu.get_barrier_semaphore()

    def greet(i, carry):
        pl.semaphore_signal(barrier, inc=1, device_id=plane(at_offset(i)), device_id_type=MESH)
        return carry

    lax.fori_loop(1, 32, greet, 0)
    up = lax.rem(z + 1, 8) * 2 + c
    down = lax.rem(z + 7, 8) * 2 + c
    for who in (up, down, other):
        pl.semaphore_signal(barrier, inc=1, device_id=(l, who), device_id_type=MESH)
    pl.semaphore_wait(barrier, 34)

    def rows_of(j):
        return pl.ds(pl.multiple_of(j * 8, 8), 8)

    def piece_src(j, f):
        return blocks.at[:, pl.ds(pl.multiple_of(place(j) * 8, 8), 8), pl.ds(f * 128, 128)]

    for f in range(2):

        def send(i, carry, f=f):
            j = peer(i, f)

            @pl.when(j != l)
            def _():
                pltpu.make_async_remote_copy(
                    src_ref=piece_src(j, f),
                    dst_ref=gathered.at[rows_of(l)],
                    send_sem=send_a,
                    recv_sem=recv_a.at[l],
                    device_id=plane(j),
                    device_id_type=MESH,
                ).start()

            @pl.when(j == l)
            def _():
                pltpu.make_async_copy(piece_src(j, f), gathered.at[rows_of(l)], local_sem).start()

            return carry

        lax.fori_loop(0, 16, send, 0)

    pltpu.make_async_copy(gathered.at[rows_of(l)], gathered.at[rows_of(l)], local_sem).wait()

    def await_a(i, carry):
        j = at_offset(i)
        pltpu.make_async_copy(gathered.at[rows_of(j)], gathered.at[rows_of(j)], recv_a.at[j]).wait()
        return carry

    lax.fori_loop(1, 32, await_a, 0)

    def sort(j, carry):
        for s in range(8):
            sorted_[j * 8 + s] = gathered[inv[j * 8 + s]]
        return carry

    lax.fori_loop(0, 32, sort, 0)

    def send_out(i, carry):
        j = at_offset(i)
        pltpu.make_async_remote_copy(
            src_ref=sorted_.at[rows_of(j)],
            dst_ref=landed.at[own_f, :, own_place],
            send_sem=send_b,
            recv_sem=recv_b.at[l],
            device_id=plane(j),
            device_id_type=MESH,
        ).start()
        return carry

    lax.fori_loop(1, 32, send_out, 0)
    for s in range(8):
        landed[own_f, s, own_place] = sorted_[l * 8 + s]

    cols = pl.ds(pl.multiple_of(z * 256, 256), 256)
    half_rows = pl.ds(pl.multiple_of(c * 64, 64), 64)
    w_src = wkv.at[half_rows, cols]
    own_w = pltpu.make_async_copy(w_src, wout.at[l, half_rows], local_sem)
    own_w.start()

    def send_wy(i, carry):
        j = x * 8 + lax.rem(y + i, 8)
        pltpu.make_async_remote_copy(
            src_ref=w_src,
            dst_ref=wout.at[l, half_rows],
            send_sem=send_w.at[0],
            recv_sem=recv_wy.at[y],
            device_id=plane(j),
            device_id_type=MESH,
        ).start()
        return carry

    lax.fori_loop(1, 8, send_wy, 0)

    def arrive(f):
        def await_b(i, carry):
            j = peer(i, f)

            @pl.when(j != l)
            def _():
                ref = landed.at[f, :, place(j)]
                pltpu.make_async_copy(ref, ref, recv_b.at[j]).wait()

            return carry

        lax.fori_loop(0, 16, await_b, 0)

        g = gain[:, f * 128 : (f + 1) * 128].astype(F32).reshape(1, 1, 128)
        row = lax.broadcasted_iota(jnp.int32, (8, 128), 0)
        ones = jnp.ones((8, 128), BF16)

        def scale(s, total):
            xv = landed[f, s].astype(F32)
            xall[z, c, f, pl.ds(s * 16, 16)] = (xv * g).astype(BF16)
            sq = (xv * xv).reshape(128, 128)
            hi = sq.astype(BF16)
            lo = (sq - hi.astype(F32)).astype(BF16)
            dims = (((1,), (1,)), ((), ()))
            sums = lax.dot_general(ones, hi, dims, preferred_element_type=F32)
            sums += lax.dot_general(ones, lo, dims, preferred_element_type=F32)
            return jnp.where(row == s, sums, total)

        total = lax.fori_loop(0, 8, scale, jnp.zeros((8, 128), F32))
        hi = total.astype(BF16)
        xall[z, c, f, 128] = hi
        xall[z, c, f, 129] = (total - hi.astype(F32)).astype(BF16)

    def part(zo, cc, f, h):
        return xall.at[zo, cc, f, pl.ds(HALF * h, HALF)]

    def to_ring(zo, f, h, way, step):
        pltpu.make_async_remote_copy(
            src_ref=part(zo, c, f, h),
            dst_ref=part(zo, c, f, h),
            send_sem=send_z,
            recv_sem=recv_z.at[f, h, way, step],
            device_id=(l, up if way == 0 else down),
            device_id_type=MESH,
        ).start()

    def to_sibling(zo, f, h, k):
        pltpu.make_async_remote_copy(
            src_ref=part(zo, c, f, h),
            dst_ref=part(zo, c, f, h),
            send_sem=send_d,
            recv_sem=recv_d.at[f, h, k],
            device_id=(l, other),
            device_id_type=MESH,
        ).start()

    def begin(f):
        for h in range(2):
            to_ring(z, f, h, 0, 0)
            to_ring(z, f, h, 1, 0)
        for h in range(2):
            to_sibling(z, f, h, 0)

    def ring(f, step):
        for h in range(2):
            for way in range(2):
                if step == 4 and way != h:
                    continue
                k = (8 - step) if way == 0 else step
                zo = lax.rem(z + k, 8)
                ref = part(zo, c, f, h)
                pltpu.make_async_copy(ref, ref, recv_z.at[f, h, way, step - 1]).wait()
                if step < 3 or (step == 3 and way == h):
                    to_ring(zo, f, h, way, step)
                to_sibling(zo, f, h, k)

    def weights_x():
        own_w.wait()

        def await_wy(i, carry):
            yy = lax.rem(y + i, 8)
            ref = wout.at[x * 8 + yy, half_rows]
            pltpu.make_async_copy(ref, ref, recv_wy.at[yy]).wait()
            return carry

        lax.fori_loop(1, 8, await_wy, 0)
        for i in range(1, 4):
            mine = wout.at[pl.ds(pl.multiple_of(x * 8, 8), 8), half_rows]
            pltpu.make_async_remote_copy(
                src_ref=mine,
                dst_ref=mine,
                send_sem=send_w.at[1],
                recv_sem=recv_wx.at[x],
                device_id=plane(lax.rem(x + i, 4) * 8 + y),
                device_id_type=MESH,
            ).start()

    def weights_sibling():
        for i in range(1, 4):
            xx = lax.rem(x + i, 4)
            ref = wout.at[pl.ds(pl.multiple_of(xx * 8, 8), 8), half_rows]
            pltpu.make_async_copy(ref, ref, recv_wx.at[xx]).wait()
        pltpu.make_async_remote_copy(
            src_ref=wout.at[:, half_rows],
            dst_ref=wout.at[:, half_rows],
            send_sem=send_w.at[2],
            recv_sem=recv_wd,
            device_id=(l, other),
            device_id_type=MESH,
        ).start()

    arrive(0)
    begin(0)
    ring(0, 1)
    weights_x()
    ring(0, 2)
    arrive(1)
    begin(1)
    ring(0, 3)
    ring(1, 1)
    ring(0, 4)
    weights_sibling()
    ring(1, 2)
    ring(1, 3)
    ring(1, 4)

    for f in range(2):
        for h in range(2):
            for k in range(8):
                ref = part(lax.rem(z + k, 8), 1 - c, f, h)
                pltpu.make_async_copy(ref, ref, recv_d.at[f, h, k]).wait()
    their = wout.at[:, pl.ds(pl.multiple_of((1 - c) * 64, 64), 64)]
    pltpu.make_async_copy(their, their, recv_wd).wait()

    def drain(ref, sem):
        pltpu.make_async_copy(ref, ref, sem).wait()

    drain(gathered.at[pl.ds(0, 248)], send_a)
    drain(gathered.at[pl.ds(0, 248)], send_b)
    drain(xall.at[pl.ds(0, 7), :, 0], send_z)
    drain(xall.at[:, :, 0], send_d)
    drain(wout.at[pl.ds(0, 7), half_rows], send_w.at[0])
    drain(wout.at[pl.ds(0, 24), half_rows], send_w.at[1])
    drain(wout.at[:, half_rows], send_w.at[2])


def compute_kernel(xt, sums, wq, wk, seg, out, keys, values, rms, segc):
    i = pl.program_id(0)

    @pl.when(i == 0)
    def _():
        keys[0:256] = jnp.zeros((256, HD), BF16)
        values[0:256] = jnp.zeros((256, HD), BF16)
        total = jnp.zeros((8, 128), F32)
        for zz in range(8):
            for cc in range(2):
                for f in range(2):
                    both = sums[zz, cc, f].astype(F32)
                    total += both[0:8] + both[8:16]
        inverse = lax.rsqrt(total / D + 1e-05).T
        doc = seg[8:16].astype(F32).T
        for r in range(8):
            rms[r] = jnp.broadcast_to(inverse[:, r : r + 1], (128, 128))
            segc[r] = jnp.broadcast_to(doc[:, r : r + 1], (128, 128))

    acc = jnp.zeros((256, 512), F32)
    for zz in range(8):
        for f in range(2):
            xs = jnp.concatenate([xt[zz, 0, f], xt[zz, 1, f]], axis=1)
            lo, hi = (zz * 2) * 256 + f * 128, (zz * 2 + 1) * 256 + f * 128
            top = jnp.concatenate([wq[lo : lo + 128], wk[zz * 4 + f]], axis=1)
            bottom = jnp.concatenate([wq[hi : hi + 128], wk[zz * 4 + 2 + f]], axis=1)
            acc += jnp.dot(xs, jnp.concatenate([top, bottom], axis=0), preferred_element_type=F32)
    r2 = jnp.concatenate([rms[2 * i], rms[2 * i + 1]], axis=0)[:, 0:1]
    acc = acc * r2
    q = acc[:, 0:256].astype(BF16)
    start = pl.multiple_of(i * 256, 256)
    keys[pl.ds(start + 256, 256)] = acc[:, 256:384].astype(BF16)
    values[pl.ds(start + 256, 256)] = acc[:, 384:512].astype(BF16)
    kw = keys[pl.ds(start, 512)]
    vw = values[pl.ds(start, 512)]
    qdoc = jnp.concatenate([segc[2 * i], segc[2 * i + 1]], axis=0)[:, 0:1]
    kdoc = jnp.concatenate([seg[pl.ds(6 + 2 * i + n, 1)] for n in range(4)], axis=1).astype(F32)
    row = lax.broadcasted_iota(jnp.int32, (256, 512), 0)
    col = lax.broadcasted_iota(jnp.int32, (256, 512), 1)
    allowed = (qdoc == kdoc) & (col <= row + 256)
    for h in range(2):
        s = lax.dot_general(
            q[:, h * HD : (h + 1) * HD], kw, (((1,), (1,)), ((), ())), preferred_element_type=F32
        )
        masked = jnp.where(allowed, s * (1.0 / math.sqrt(HD)), -1e30)
        top = jnp.max(masked, axis=-1, keepdims=True)
        e = jnp.where(allowed, jnp.exp(masked - top), 0.0)
        p = (e * (1.0 / jnp.sum(e, axis=-1, keepdims=True))).astype(BF16)
        out[:, h * HD : (h + 1) * HD] = jnp.dot(p, vw, preferred_element_type=F32).astype(BF16)


def on_device(blocks, seg_ids, dest, slot, norm_gain, w_query, w_keyval):
    ids = jnp.arange(256, dtype=jnp.int32)
    position = dest * 8 + slot
    inv = jnp.sum(jnp.where(position[None, :] == ids[:, None], ids[None, :], 0), axis=1)
    dma = pltpu.SemaphoreType.DMA
    anywhere = pl.BlockSpec(memory_space=pl.ANY)
    vmem = pl.BlockSpec(memory_space=pltpu.VMEM)
    xall, wk = pl.pallas_call(
        comm_kernel,
        out_shape=(
            jax.ShapeDtypeStruct((8, 2, 2, TILES, 8, 128), BF16),
            jax.ShapeDtypeStruct((32, 128, 256), BF16),
        ),
        in_specs=[pl.BlockSpec(memory_space=pltpu.SMEM), anywhere, vmem, anywhere],
        out_specs=(vmem, vmem),
        scratch_shapes=[
            pltpu.VMEM((256, 8, 128), BF16),
            pltpu.VMEM((256, 8, 128), BF16),
            pltpu.VMEM((2, 8, 16, 8, 128), BF16),
            dma, dma, dma((32,)), dma, dma((32,)),
            dma, dma((2, 2, 2, 4)), dma, dma((2, 2, 8)),
            dma((3,)), dma((8,)), dma((4,)), dma,
        ],
        compiler_params=pltpu.CompilerParams(
            collective_id=0, has_side_effects=True, vmem_limit_bytes=40 * 1024 * 1024
        ),
        name="exchange",
    )(inv.astype(jnp.int32), blocks, norm_gain.reshape(1, 256), w_keyval)
    xall = xall.reshape(8, 2, 2, TILES * 8, 128)
    rows = seg_ids.reshape(8, 128)
    seg = jnp.concatenate([jnp.full((8, 128), -1, jnp.int32), rows], axis=0)
    return pl.pallas_call(
        compute_kernel,
        grid=(4,),
        out_shape=jax.ShapeDtypeStruct((1024, 256), BF16),
        in_specs=[
            pl.BlockSpec((8, 2, 2, 256, 128), lambda i: (0, 0, 0, i, 0)),
            pl.BlockSpec((8, 2, 2, 16, 128), lambda i: (0, 0, 0, 64, 0)),
            pl.BlockSpec((4096, 256), lambda i: (0, 0)),
            pl.BlockSpec((32, 128, 256), lambda i: (0, 0, 0)),
            pl.BlockSpec((16, 128), lambda i: (0, 0)),
        ],
        out_specs=pl.BlockSpec((256, 256), lambda i: (i, 0)),
        scratch_shapes=[
            pltpu.VMEM((1280, HD), BF16),
            pltpu.VMEM((1280, HD), BF16),
            pltpu.VMEM((8, 128, 128), F32),
            pltpu.VMEM((8, 128, 128), F32),
        ],
        compiler_params=pltpu.CompilerParams(
            dimension_semantics=("arbitrary",), vmem_limit_bytes=40 * 1024 * 1024
        ),
        name="project_attend",
    )(xall, xall, w_query, wk, seg)


def solution(mesh):
    return jax.shard_map(
        on_device,
        mesh=mesh,
        in_specs=(
            P("learner", None, "tensor"),
            P("learner", None),
            P(),
            P(),
            P("tensor"),
            P(None, "tensor"),
            P("learner", None),
        ),
        out_specs=P("learner", "tensor"),
        check_vma=False,
    )
```

time: 197 us -> 108 us (0.55)
  waiting for transfers between devices: 111 us -> 0 us
  Pallas kernels: 0 us -> 101 us
  matrix products: 21 us -> 0 us
  starting transfers between devices: 18.1 us -> 0 us
  between operations: 13.6 us -> 0.02 us
  other arithmetic: 12.5 us -> 0.81 us
  local copies, waits for them, and re-layouts: 15.7 us -> 5.02 us
  loops' own time: 4.2 us -> 0 us
    pallas_call x0 -> x2, Pallas kernels: none -> 101 us  [the longest x1 88.6 us: on_device(): pl.pallas_call(comm_kernel, out_shape=(jax.ShapeDtypeStruct((8, 2, 2, TIL...]
    all_gather x1 -> x0, waiting for transfers between devices: 62.6 us -> none  [in_one_piece(): lax.all_gather(both, axis, axis=dim, tiled=True)]
    all_to_all x2 -> x0, waiting for transfers between devices: 48.6 us -> none  [the longest x1 48.6 us: on_device(): lax.all_to_all(outgoing, 'learner', split_axis=0, concat_axis=0, tiled=True)]
    dot_general x8 -> x0, matrix products: 21 us -> none  [the longest x1 6.63 us: on_device(): jnp.dot(normed, kv_weight, preferred_element_type=jnp.float32)]
    all_to_all x2 -> x0, starting transfers between devices: 18.1 us -> none  [the longest x1 10.7 us: on_device(): lax.all_to_all(outgoing, 'learner', split_axis=0, concat_axis=0, tiled=True)]
    dot_general x1 -> x0, other arithmetic: 5.07 us -> none  [on_device(): jnp.einsum('rd,rd->r', whole_rows, whole_rows, preferred_element_type=jnp...]
    another operation x1 -> x0, loops' own time: 4.2 us -> none  [on_device(): result = lax.map(attend, (query_parts, starts))]
    unnamed x14 -> x6, local copies, waits for them, and re-layouts: 7.42 us -> 3.67 us
  transfers between devices with their start and end apart: 3 -> 0, of which waited for: 2 -> 0; matrix products, arithmetic and copies ran while one was open for 4% -> 0% of each run, Pallas kernels for 0% -> 0%
where the time goes in v1:
time: 108 us; the launch traced here: 107 us
  Pallas kernels  101 us (94%)
  local copies, waits for them, and re-layouts  5.02 us (5%)
    pallas_call x1, Pallas kernels, on_device(): pl.pallas_call(comm_kernel, out_shape=(jax.ShapeDtypeStruct((8, 2, 2, TIL...  88.6 us
    pallas_call x1, Pallas kernels, on_device(): pl.pallas_call(compute_kernel, grid=(4,), out_shape=jax.ShapeDtypeStruct(...  12.2 us
    unnamed x6, local copies, waits for them, and re-layouts  3.67 us

profile of v1, /device:TPU:1, one launch (start us, length us, event | category | flops | bytes accessed | tf_op | source)
XLA Modules:
  0.0 106.7 jit_solution(11624397665793056392)
XLA Ops:
  0.0 0.7 multiply_add_fusion
  0.7 0.1 select_reduce_fusion.inv
  0.8 0.7 reshape.10.gain
  1.5 0.7 concatenate.3.seg
  2.2 0.0 copy-start.1
  2.2 1.0 copy-done.1
  3.2 0.0 copy-start.2
  3.2 1.0 copy-done.2
  4.3 88.6 %exchange.1 = (bf16[8,2,2,130,8,128]{5,4,3,2,1,0:T(8,128)(2,1)S(1)}, bf16[32,128,256]{2,1,0:T(8,128)(2,1)S(1)}) custom-call(s32[256]{0:T(256)S(1)} %select_reduce_fusion.inv, bf16[8,128,256]{2,1,0:T(8,128)(2,1)S(1)} %copy-done.1, bf16[1,256]{1,0:T(2,128)(2,1)S(1)} %reshape.10.gain, bf16[128,2048]{1,0:T(8,128)(2,1)S(1)} %copy-done.2), custom_call_target="tpu_custom_call" | custom-call | tf_op jit(solution)/shard_map/exchange/pallas_call | solution.py:349
  92.8 0.0 copy-start
  92.9 1.6 %copy-done = bf16[4096,256]{1,0:T(8,128)(2,1)S(1)} copy-done((bf16[4096,256]{1,0:T(8,128)(2,1)S(1)}, bf16[4096,256]{1,0:T(8,128)(2,1)}, u32[]{:S(2)}) %copy-start) | copy-done | bytes 2097176
  94.4 12.2 %project_attend.1 = bf16[1024,256]{1,0:T(8,128)(2,1)} custom-call(bf16[8,2,2,1040,128]{4,3,2,1,0:T(8,128)(2,1)S(1)} %bitcast.2, bf16[8,2,2,1040,128]{4,3,2,1,0:T(8,128)(2,1)S(1)} %bitcast.3, bf16[4096,256]{1,0:T(8,128)(2,1)S(1)} %copy-done, bf16[32,128,256]{2,1,0:T(8,128)(2,1)S(1)} %get-tuple-element.8.wk, s32[16,128]{1,0:T(8,128)S(1)} %concatenate.3.seg), custom_call_target="tpu_custom_call" | custom-call | tf_op jit(solution)/shard_map/project_attend/pallas_call | solution.py:373
Async XLA Ops:
  2.2 1.0 copy-start.1
  3.2 1.0 copy-start.2
  92.8 1.6 %copy-start = (bf16[4096,256]{1,0:T(8,128)(2,1)S(1)}, bf16[4096,256]{1,0:T(8,128)(2,1)}, u32[]{:S(2)}) copy-start(bf16[4096,256]{1,0:T(8,128)(2,1)} %wq.1) | copy-start | bytes 6291460

commit v2 on v0

v2 whole, which is shorter than its diff:
```python
import math

import jax
import jax.numpy as jnp
from jax import lax
from jax.experimental import pallas as pl
from jax.experimental.pallas import tpu as pltpu
from jax.sharding import PartitionSpec as P

D = 4096
HD = 128
MESH = pl.DeviceIdType.MESH
F32 = jnp.float32
BF16 = jnp.bfloat16
I32 = jnp.int32
ROWS = 528


def exchange_kernel(
    dest, slot, blocks, gain, wkv, wq, out,
    own, gathered, sorted_, landed, xall, wk, wq_v, acc, ready, inv_v, inv,
    own_sem, wq_sem, inv_sem, out_sem, w_sem,
    send_a, recv_a, send_b, recv_b, send_z, recv_z, send_d, recv_d,
    send_w, recv_wy, recv_wx, recv_wd,
):
    l = lax.axis_index("learner")
    t = lax.axis_index("tensor")
    x, y = lax.div(l, 8), lax.rem(l, 8)
    z, c = lax.div(t, 2), lax.rem(t, 2)
    other = z * 2 + (1 - c)
    up = lax.rem(z + 1, 8) * 2 + c
    down = lax.rem(z + 7, 8) * 2 + c

    def at_offset(i):
        return lax.rem(x + lax.div(i, 8), 4) * 8 + lax.rem(y + lax.rem(i, 8), 8)

    def peer(i, q):
        return lax.rem(x + lax.div(i, 2), 4) * 8 + lax.rem(lax.div(y, 4) + lax.rem(i, 2), 2) * 4 + q

    def place(j):
        return lax.div(j, 8) * 2 + lax.div(lax.rem(j, 8), 4)

    def pending(ref, sem):
        return pltpu.make_async_copy(ref, ref, sem)

    own_q = lax.rem(y, 4)
    own_place = place(l)

    barrier = pltpu.get_barrier_semaphore()

    def greet(i, carry):
        pl.semaphore_signal(barrier, inc=1, device_id=(at_offset(i), t), device_id_type=MESH)
        return carry

    lax.fori_loop(1, 32, greet, 0)
    for who in (up, down, other):
        pl.semaphore_signal(barrier, inc=1, device_id=(l, who), device_id_type=MESH)

    take_own = pltpu.make_async_copy(blocks, own, own_sem)
    take_own.start()
    take_wq = pltpu.make_async_copy(wq, wq_v, wq_sem)
    take_wq.start()
    position = dest[...] * 8 + slot[...]
    column = jnp.concatenate([position] * 4, axis=0).T
    where_to = lax.broadcasted_iota(I32, (128, 256), 1)
    who_from = lax.broadcasted_iota(I32, (128, 256), 0)
    table = jnp.zeros((1, 256), I32)
    for k in range(2):
        hit = column[:, k : k + 1] == where_to
        found = jnp.max(jnp.where(hit, who_from + 128 * k, 0), axis=0, keepdims=True)
        table = jnp.maximum(table, found)
    inv_v[...] = table
    take_inv = pltpu.make_async_copy(inv_v, inv, inv_sem)
    take_inv.start()
    take_own.wait()
    pl.semaphore_wait(barrier, 34)

    def rows_of(j):
        return pl.ds(pl.multiple_of(j * 8, 8), 8)

    for q in range(4):

        def send(i, carry, q=q):
            j = peer(i, q)
            src = own.at[:, 8 * (q % 2) + place(j), :, pl.ds((q // 2) * 128, 128)]

            @pl.when(j != l)
            def _():
                pltpu.make_async_remote_copy(
                    src_ref=src,
                    dst_ref=gathered.at[rows_of(l)],
                    send_sem=send_a,
                    recv_sem=recv_a.at[l],
                    device_id=(j, t),
                    device_id_type=MESH,
                ).start()

            @pl.when(j == l)
            def _():
                for b in range(8):
                    gathered[l * 8 + b] = own[b, 8 * (q % 2) + place(j), :, (q // 2) * 128 : (q // 2) * 128 + 128]

            return carry

        lax.fori_loop(0, 8, send, 0)

    take_inv.wait()

    def await_a(i, carry):
        j = at_offset(i)
        pending(gathered.at[rows_of(j)], recv_a.at[j]).wait()
        return carry

    lax.fori_loop(1, 32, await_a, 0)

    def sort(j, carry):
        for s in range(8):
            sorted_[j * 8 + s] = gathered[inv[0, j * 8 + s]]
        return carry

    lax.fori_loop(0, 32, sort, 0)

    def send_out(i, carry):
        j = at_offset(i)
        pltpu.make_async_remote_copy(
            src_ref=sorted_.at[rows_of(j)],
            dst_ref=landed.at[own_q, :, own_place],
            send_sem=send_b,
            recv_sem=recv_b.at[l],
            device_id=(j, t),
            device_id_type=MESH,
        ).start()
        return carry

    lax.fori_loop(1, 32, send_out, 0)
    for s in range(8):
        landed[own_q, s, own_place] = sorted_[l * 8 + s]

    half_rows = pl.ds(pl.multiple_of(c * 64, 64), 64)
    w_src = wkv.at[half_rows, pl.ds(pl.multiple_of(z * 256, 256), 256)]
    take_w = pltpu.make_async_copy(w_src, wk.at[l, half_rows], w_sem)
    take_w.start()

    def send_wy(i, carry):
        pltpu.make_async_remote_copy(
            src_ref=w_src,
            dst_ref=wk.at[l, half_rows],
            send_sem=send_w.at[0],
            recv_sem=recv_wy.at[y],
            device_id=(x * 8 + lax.rem(y + i, 8), t),
            device_id_type=MESH,
        ).start()
        return carry

    lax.fori_loop(1, 8, send_wy, 0)

    def weights_x():
        take_w.wait()

        def await_wy(i, carry):
            yy = lax.rem(y + i, 8)
            pending(wk.at[x * 8 + yy, half_rows], recv_wy.at[yy]).wait()
            return carry

        lax.fori_loop(1, 8, await_wy, 0)
        for way in range(2):
            to_column(x, 8, 0, way)

    def column(xx, first, count):
        return wk.at[pl.ds(pl.multiple_of(xx * 8 + first, 4), count), half_rows]

    def to_column(xx, count, first, way):
        ref = column(xx, first, count)
        pltpu.make_async_remote_copy(
            src_ref=ref,
            dst_ref=ref,
            send_sem=send_w.at[1],
            recv_sem=recv_wx.at[way, 0 if count == 8 else 1],
            device_id=(lax.rem(x + (1 if way == 0 else 3), 4) * 8 + y, t),
            device_id_type=MESH,
        ).start()

    def weights_x2():
        for way in range(2):
            xx = lax.rem(x + (3 if way == 0 else 1), 4)
            pending(column(xx, 0, 8), recv_wx.at[way, 0]).wait()
            to_column(xx, 4, 4 * way, way)

    def weights_sibling():
        xx = lax.rem(x + 2, 4)
        for way in range(2):
            pending(column(xx, 4 * way, 4), recv_wx.at[way, 1]).wait()
        mine = wk.at[:, half_rows]
        pltpu.make_async_remote_copy(
            src_ref=mine,
            dst_ref=mine,
            send_sem=send_w.at[2],
            recv_sem=recv_wd,
            device_id=(l, other),
            device_id_type=MESH,
        ).start()

    def weights_ready():
        pending(wk.at[:, pl.ds(pl.multiple_of((1 - c) * 64, 64), 64)], recv_wd).wait()

    row = lax.broadcasted_iota(I32, (8, 128), 0)

    def arrive(q):
        def await_b(i, carry):
            j = peer(i, q)

            @pl.when(j != l)
            def _():
                pending(landed.at[q, :, place(j)], recv_b.at[j]).wait()

            return carry

        lax.fori_loop(0, 8, await_b, 0)
        f = q // 2
        g = gain[f * 128 : (f + 1) * 128].astype(F32).reshape(1, 128)
        ones = jnp.ones((8, 128), BF16)
        dims = (((1,), (1,)), ((), ()))

        def scale(j, total):
            xv = landed[q, pl.ds(2 * j, 2)].astype(F32).reshape(128, 128)
            xall[z, c, q, pl.ds(pl.multiple_of(j * 128, 128), 128)] = (xv * g).astype(BF16)
            sq = xv * xv
            hi = sq.astype(BF16)
            lo = (sq - hi.astype(F32)).astype(BF16)
            sums = lax.dot_general(ones, hi, dims, preferred_element_type=F32)
            sums += lax.dot_general(ones, lo, dims, preferred_element_type=F32)
            return jnp.where(lax.rem(row, 4) == j, sums, total)

        total = lax.fori_loop(0, 4, scale, jnp.zeros((8, 128), F32))
        hi = total.astype(BF16).astype(F32)
        tile = jnp.where(row < 4, hi, total - hi)
        xall[z, c, q, 512:528] = jnp.concatenate([tile, jnp.zeros((8, 128), F32)], axis=0).astype(BF16)

    def to_ring(zo, q, way, step):
        pltpu.make_async_remote_copy(
            src_ref=xall.at[zo, c, q],
            dst_ref=xall.at[zo, c, q],
            send_sem=send_z,
            recv_sem=recv_z.at[q, way, step],
            device_id=(l, up if way == 0 else down),
            device_id_type=MESH,
        ).start()

    def to_sibling(zo, q, k):
        pltpu.make_async_remote_copy(
            src_ref=xall.at[zo, c, q],
            dst_ref=xall.at[zo, c, q],
            send_sem=send_d,
            recv_sem=recv_d.at[q, k],
            device_id=(l, other),
            device_id_type=MESH,
        ).start()

    def begin(q):
        to_ring(z, q, 0, 0)
        to_ring(z, q, 1, 0)
        to_sibling(z, q, 0)

    def ring(q, step):
        for way in range(2):
            if step == 4 and way != q % 2:
                continue
            k = (8 - step) if way == 0 else step
            zo = lax.rem(z + k, 8)
            pending(xall.at[zo, c, q], recv_z.at[q, way, step - 1]).wait()
            if step < 3 or (step == 3 and way == q % 2):
                to_ring(zo, q, way, step)
            to_sibling(zo, q, k)

    def project(kind, q, first, second):
        f, half = q // 2, q % 2
        zs = [lax.rem(z + k, 8) for k in (first, second)]
        if kind == 0:
            for k, zo in zip((first, second), zs):
                pending(xall.at[zo, 1 - c, q], recv_d.at[q, k]).wait()

        def some_rows(i, carry):
            start = pl.multiple_of(i * 256, 256)
            pairs = [(zo, cc) for zo in zs for cc in range(2)]
            lhs = jnp.concatenate([xall[zo, cc, q, pl.ds(start, 256)] for zo, cc in pairs], axis=1)
            if kind == 0:
                rhs = [wq_v[pl.ds(pl.multiple_of(zo * 512 + cc * 256 + f * 128, 128), 128)] for zo, cc in pairs]
            else:
                rhs = [wk[zo * 4 + cc * 2 + f] for zo, cc in pairs]
            got = jnp.dot(lhs, jnp.concatenate(rhs, axis=0), preferred_element_type=F32)
            at = pl.ds(pl.multiple_of(half * 512 + start, 256), 256)
            if f == 0 and first == 1:
                acc[kind, at] = got
            else:
                acc[kind, at] += got
            return carry

        lax.fori_loop(0, 2, some_rows, 0)

    for q in range(4):
        arrive(q)
        begin(q)
    weights_x()
    for q in range(4):
        ring(q, 1)
    weights_x2()
    take_wq.wait()
    for q in range(4):
        ring(q, 2)
        project(0, q, 1, 7)
    weights_sibling()
    for q in range(4):
        ring(q, 3)
        project(0, q, 2, 6)
    weights_ready()
    project(1, 0, 1, 7)
    project(1, 1, 1, 7)
    project(1, 2, 1, 7)
    ring(0, 4)
    project(1, 3, 1, 7)
    project(1, 0, 2, 6)
    project(1, 1, 2, 6)
    project(0, 0, 3, 5)
    project(1, 0, 3, 5)
    ring(1, 4)
    project(1, 2, 2, 6)
    project(1, 3, 2, 6)
    project(0, 1, 3, 5)
    project(1, 1, 3, 5)
    project(0, 2, 3, 5)
    ring(2, 4)
    project(1, 2, 3, 5)
    project(0, 3, 3, 5)
    project(1, 3, 3, 5)
    project(0, 0, 0, 4)
    ring(3, 4)
    project(1, 0, 0, 4)
    for q in range(1, 4):
        project(0, q, 0, 4)
        project(1, q, 0, 4)

    sums = []
    for half in range(2):
        total = jnp.zeros((8, 128), F32)
        for zz in range(8):
            for cc in range(2):
                for f in range(2):
                    total += xall[zz, cc, 2 * f + half, 512:528].astype(F32)[0:8]
        sums.append(total[0:4] + total[4:8])
    inverse = lax.rsqrt(jnp.concatenate(sums, axis=0) / D + 1e-05).T
    results = []
    for j in range(4):
        for half in range(2):
            start = half * 512 + j * 128
            factor = inverse[:, half * 4 + j : half * 4 + j + 1]
            for kind in range(2):
                scaled = (acc[kind, start : start + 128] * factor).astype(BF16)
                for e in range(2):
                    to = (2 * j + e) * 128 + half * 64
                    ready[to : to + 64, kind * 256 : kind * 256 + 256] = scaled[e * 64 : e * 64 + 64]
        at = pl.ds(256 * j, 256)
        result = pltpu.make_async_copy(ready.at[at], out.at[at], out_sem.at[j])
        result.start()
        results.append(result)

    pending(gathered.at[pl.ds(0, 248)], send_a).wait()
    pending(gathered.at[pl.ds(0, 248)], send_b).wait()
    pending(xall.at[pl.ds(0, 7), 0], send_z).wait()
    pending(xall.at[:, 0], send_d).wait()
    pending(wk.at[pl.ds(0, 7), half_rows], send_w.at[0]).wait()
    pending(wk.at[pl.ds(0, 24), half_rows], send_w.at[1]).wait()
    pending(wk.at[:, half_rows], send_w.at[2]).wait()
    for result in results:
        result.wait()


def attend_kernel(qkv, seg, out, held, buf, take_sem, sems):
    takes = []
    for i in range(4):
        at = pl.ds(256 * i, 256)
        take = pltpu.make_async_copy(qkv.at[at], held.at[at], take_sem.at[i])
        take.start()
        takes.append(take)
    docs = seg[...].astype(F32)
    columns = jnp.concatenate([docs[:, r * 128 : r * 128 + 128] for r in range(8)], axis=0).T
    copies = []
    for i in range(4):
        start, begin = 256 * i, max(0, 256 * i - 256)
        width = start + 256 - begin
        qdoc = jnp.concatenate([columns[:, 2 * i : 2 * i + 1], columns[:, 2 * i + 1 : 2 * i + 2]], axis=0)
        row = lax.broadcasted_iota(I32, (256, width), 0)
        col = lax.broadcasted_iota(I32, (256, width), 1)
        allowed = (qdoc == docs[:, begin : begin + width]) & (col <= row + (start - begin))
        takes[i].wait()
        keys = held[begin : begin + width, 2 * HD : 3 * HD]
        values = held[begin : begin + width, 3 * HD : 4 * HD]
        for h in range(2):
            s = lax.dot_general(
                held[start : start + 256, h * HD : (h + 1) * HD], keys, (((1,), (1,)), ((), ())),
                preferred_element_type=F32,
            )
            masked = jnp.where(allowed, s, -1e30)
            top = jnp.max(masked, axis=-1, keepdims=True)
            e = jnp.exp2((masked - top) * (math.log2(math.e) / math.sqrt(HD)))
            part = jnp.dot(e.astype(BF16), values, preferred_element_type=F32)
            part = part * (1.0 / jnp.sum(e, axis=-1, keepdims=True))
            buf[start : start + 256, h * HD : (h + 1) * HD] = part.astype(BF16)
        at = pl.ds(start, 256)
        copy = pltpu.make_async_copy(buf.at[at], out.at[at], sems.at[i])
        copy.start()
        copies.append(copy)
    for copy in copies:
        copy.wait()


def on_device(blocks, seg_ids, dest, slot, norm_gain, w_query, w_keyval):
    dma = pltpu.SemaphoreType.DMA
    hbm = pl.BlockSpec(memory_space=pltpu.HBM)
    vmem = pl.BlockSpec(memory_space=pltpu.VMEM)
    qkv = pl.pallas_call(
        exchange_kernel,
        out_shape=jax.ShapeDtypeStruct((1024, 512), BF16),
        in_specs=[vmem, vmem, hbm, vmem, hbm, hbm],
        out_specs=hbm,
        scratch_shapes=[
            pltpu.VMEM((8, 16, 8, 256), BF16),
            pltpu.VMEM((256, 8, 128), BF16),
            pltpu.VMEM((256, 8, 128), BF16),
            pltpu.VMEM((4, 8, 8, 8, 128), BF16),
            pltpu.VMEM((8, 2, 4, ROWS, 128), BF16),
            pltpu.VMEM((32, 128, 256), BF16),
            pltpu.VMEM((4096, 256), BF16),
            pltpu.VMEM((2, 1024, 256), F32),
            pltpu.VMEM((1024, 512), BF16),
            pltpu.VMEM((1, 256), I32),
            pltpu.SMEM((1, 256), I32),
            dma, dma, dma, dma((4,)), dma,
            dma, dma((32,)), dma, dma((32,)), dma, dma((4, 2, 4)), dma, dma((4, 8)),
            dma((3,)), dma((8,)), dma((2, 2)), dma,
        ],
        compiler_params=pltpu.CompilerParams(
            collective_id=0, has_side_effects=True, vmem_limit_bytes=60 * 1024 * 1024
        ),
        name="exchange",
    )(
        dest.reshape(2, 128),
        slot.reshape(2, 128),
        blocks.reshape(8, 16, 8, 256),
        norm_gain,
        w_keyval,
        w_query,
    )
    return pl.pallas_call(
        attend_kernel,
        out_shape=jax.ShapeDtypeStruct((1024, 256), BF16),
        in_specs=[hbm, vmem],
        out_specs=hbm,
        scratch_shapes=[pltpu.VMEM((1024, 512), BF16), pltpu.VMEM((1024, 256), BF16), dma((4,)), dma((4,))],
        compiler_params=pltpu.CompilerParams(vmem_limit_bytes=60 * 1024 * 1024),
        name="attend",
    )(qkv, seg_ids)


def solution(mesh):
    return jax.shard_map(
        on_device,
        mesh=mesh,
        in_specs=(
            P("learner", None, "tensor"),
            P("learner", None),
            P(),
            P(),
            P("tensor"),
            P(None, "tensor"),
            P("learner", None),
        ),
        out_specs=P("learner", "tensor"),
        check_vma=False,
    )
```

time: 197 us -> 100 us (0.51)
  waiting for transfers between devices: 111 us -> 0 us
  Pallas kernels: 0 us -> 100 us
  matrix products: 21 us -> 0 us
  starting transfers between devices: 18.1 us -> 0 us
  local copies, waits for them, and re-layouts: 15.7 us -> 0 us
  between operations: 13.6 us -> 0.01 us
  other arithmetic: 12.5 us -> 0 us
  loops' own time: 4.2 us -> 0 us
    pallas_call x0 -> x2, Pallas kernels: none -> 100 us  [the longest x1 94.6 us: on_device(): pl.pallas_call(exchange_kernel, out_shape=jax.ShapeDtypeStruct((1024, 512...]
    all_gather x1 -> x0, waiting for transfers between devices: 62.6 us -> none  [in_one_piece(): lax.all_gather(both, axis, axis=dim, tiled=True)]
    all_to_all x2 -> x0, waiting for transfers between devices: 48.6 us -> none  [the longest x1 48.6 us: on_device(): lax.all_to_all(outgoing, 'learner', split_axis=0, concat_axis=0, tiled=True)]
    dot_general x8 -> x0, matrix products: 21 us -> none  [the longest x1 6.63 us: on_device(): jnp.dot(normed, kv_weight, preferred_element_type=jnp.float32)]
    all_to_all x2 -> x0, starting transfers between devices: 18.1 us -> none  [the longest x1 10.7 us: on_device(): lax.all_to_all(outgoing, 'learner', split_axis=0, concat_axis=0, tiled=True)]
    unnamed x14 -> x0, local copies, waits for them, and re-layouts: 7.42 us -> none
    dot_general x1 -> x0, other arithmetic: 5.07 us -> none  [on_device(): jnp.einsum('rd,rd->r', whole_rows, whole_rows, preferred_element_type=jnp...]
    another operation x1 -> x0, loops' own time: 4.2 us -> none  [on_device(): result = lax.map(attend, (query_parts, starts))]
  transfers between devices with their start and end apart: 3 -> 0, of which waited for: 2 -> 0; matrix products, arithmetic and copies ran while one was open for 4% -> 0% of each run, Pallas kernels for 0% -> 0%
where the time goes in v2:
time: 100 us
  Pallas kernels  100 us (100%)
    pallas_call x1, Pallas kernels, on_device(): pl.pallas_call(exchange_kernel, out_shape=jax.ShapeDtypeStruct((1024, 512...  94.6 us
    pallas_call x1, Pallas kernels, on_device(): pl.pallas_call(attend_kernel, out_shape=jax.ShapeDtypeStruct((1024, 256),...  5.44 us

profile of v2, /device:TPU:1, one launch (start us, length us, event | category | flops | bytes accessed | tf_op | source)
XLA Modules:
  0.0 100.0 jit_solution(8834831721457228182)
XLA Ops:
  0.0 94.6 %exchange.1.qkv = bf16[1024,512]{1,0:T(8,128)(2,1)} custom-call(s32[2,128]{1,0:T(2,128)} %bitcast.4, s32[2,128]{1,0:T(2,128)} %bitcast.5, bf16[8,16,8,256]{3,2,1,0:T(8,128)(2,1)} %bitcast.3, bf16[256]{0:T(256)(128)(2,1)} %gain.1, bf16[128,2048]{1,0:T(8,128)(2,1)} %wkv.1, bf16[4096,256]{1,0:T(8,128)(2,1)} %wq.1), custom_call_target="tpu_custom_call" | custom-call | tf_op jit(solution)/shard_map/exchange/pallas_call | solution.py:420
  94.6 5.4 %attend.1 = bf16[1024,256]{1,0:T(8,128)(2,1)} custom-call(bf16[1024,512]{1,0:T(8,128)(2,1)} %exchange.1.qkv, s32[1,1024]{1,0:T(1,128)} %seg.1), custom_call_target="tpu_custom_call" | custom-call | tf_op jit(solution)/shard_map/attend/pallas_call | solution.py:453

commit v3 on v2

--- a/solution.py
+++ b/solution.py
@@ -78,9 +78,8 @@
     def rows_of(j):
         return pl.ds(pl.multiple_of(j * 8, 8), 8)
 
-    for q in range(4):
-
-        def send(i, carry, q=q):
+    def scatter(q):
+        def send(i, carry):
             j = peer(i, q)
             src = own.at[:, 8 * (q % 2) + place(j), :, pl.ds((q // 2) * 128, 128)]
 
@@ -104,6 +103,10 @@
 
         lax.fori_loop(0, 8, send, 0)
 
+    scatter(0)
+    scatter(1)
+    scatter(2)
+    scatter(3)
     take_inv.wait()
 
     def await_a(i, carry):
@@ -111,14 +114,10 @@
         pending(gathered.at[rows_of(j)], recv_a.at[j]).wait()
         return carry
 
-    lax.fori_loop(1, 32, await_a, 0)
-
     def sort(j, carry):
         for s in range(8):
             sorted_[j * 8 + s] = gathered[inv[0, j * 8 + s]]
         return carry
-
-    lax.fori_loop(0, 32, sort, 0)
 
     def send_out(i, carry):
         j = at_offset(i)
@@ -132,9 +131,12 @@
         ).start()
         return carry
 
-    lax.fori_loop(1, 32, send_out, 0)
-    for s in range(8):
-        landed[own_q, s, own_place] = sorted_[l * 8 + s]
+    def distribute():
+        lax.fori_loop(1, 32, await_a, 0)
+        lax.fori_loop(0, 32, sort, 0)
+        lax.fori_loop(1, 32, send_out, 0)
+        for s in range(8):
+            landed[own_q, s, own_place] = sorted_[l * 8 + s]
 
     half_rows = pl.ds(pl.multiple_of(c * 64, 64), 64)
     w_src = wkv.at[half_rows, pl.ds(pl.multiple_of(z * 256, 256), 256)]
@@ -151,8 +153,6 @@
             device_id_type=MESH,
         ).start()
         return carry
-
-    lax.fori_loop(1, 8, send_wy, 0)
 
     def weights_x():
         take_w.wait()
@@ -272,81 +272,91 @@
                 to_ring(zo, q, way, step)
             to_sibling(zo, q, k)
 
-    def project(kind, q, first, second):
+    def project(kind, q, group):
         f, half = q // 2, q % 2
-        zs = [lax.rem(z + k, 8) for k in (first, second)]
+        zs = [lax.rem(z + k, 8) for k in group]
         if kind == 0:
-            for k, zo in zip((first, second), zs):
+            for k, zo in zip(group, zs):
                 pending(xall.at[zo, 1 - c, q], recv_d.at[q, k]).wait()
 
-        def some_rows(i, carry):
-            start = pl.multiple_of(i * 256, 256)
-            pairs = [(zo, cc) for zo in zs for cc in range(2)]
-            lhs = jnp.concatenate([xall[zo, cc, q, pl.ds(start, 256)] for zo, cc in pairs], axis=1)
-            if kind == 0:
-                rhs = [wq_v[pl.ds(pl.multiple_of(zo * 512 + cc * 256 + f * 128, 128), 128)] for zo, cc in pairs]
-            else:
-                rhs = [wk[zo * 4 + cc * 2 + f] for zo, cc in pairs]
-            got = jnp.dot(lhs, jnp.concatenate(rhs, axis=0), preferred_element_type=F32)
-            at = pl.ds(pl.multiple_of(half * 512 + start, 256), 256)
-            if f == 0 and first == 1:
-                acc[kind, at] = got
-            else:
-                acc[kind, at] += got
-            return carry
-
-        lax.fori_loop(0, 2, some_rows, 0)
-
+        pairs = [(zo, cc) for zo in zs for cc in range(2)]
+        lhs = jnp.concatenate([xall[zo, cc, q, 0:512] for zo, cc in pairs], axis=1)
+        if kind == 0:
+            rhs = [wq_v[pl.ds(pl.multiple_of(zo * 512 + cc * 256 + f * 128, 128), 128)] for zo, cc in pairs]
+        else:
+            rhs = [wk[zo * 4 + cc * 2 + f] for zo, cc in pairs]
+        got = jnp.dot(lhs, jnp.concatenate(rhs, axis=0), preferred_element_type=F32)
+        at = pl.ds(half * 512, 512)
+        if f == 0 and group is NEAR:
+            acc[kind, at] = got
+        else:
+            acc[kind, at] += got
+
+    def add_sums(ks):
+        for half in range(2):
+            total = jnp.zeros((8, 128), F32)
+            for k in ks:
+                for cc in range(2):
+                    for f in range(2):
+                        total += xall[lax.rem(z + k, 8), cc, 2 * f + half, 512:528].astype(F32)[0:8]
+            sums[half] = total if sums[half] is None else sums[half] + total
+
+    NEAR, MIDDLE, FAR, LAST = (0, 1, 7), (2, 6), (3, 5), (4,)
+    sums = [None, None]
+    distribute()
     for q in range(4):
         arrive(q)
         begin(q)
-    weights_x()
+    lax.fori_loop(1, 8, send_wy, 0)
     for q in range(4):
         ring(q, 1)
+    weights_x()
+    take_wq.wait()
+    ring(0, 2)
+    project(0, 0, NEAR)
+    ring(1, 2)
+    project(0, 1, NEAR)
     weights_x2()
-    take_wq.wait()
-    for q in range(4):
-        ring(q, 2)
-        project(0, q, 1, 7)
+    ring(2, 2)
+    project(0, 2, NEAR)
+    ring(3, 2)
     weights_sibling()
-    for q in range(4):
-        ring(q, 3)
-        project(0, q, 2, 6)
+    project(0, 3, NEAR)
+    ring(0, 3)
+    project(0, 0, MIDDLE)
+    project(0, 1, MIDDLE)
+    ring(1, 3)
     weights_ready()
-    project(1, 0, 1, 7)
-    project(1, 1, 1, 7)
-    project(1, 2, 1, 7)
+    project(1, 0, NEAR)
+    project(1, 1, NEAR)
+    project(1, 2, NEAR)
+    ring(2, 3)
+    project(1, 3, NEAR)
+    project(1, 0, MIDDLE)
+    project(1, 1, MIDDLE)
+    project(0, 2, MIDDLE)
+    ring(3, 3)
+    project(1, 2, MIDDLE)
+    project(0, 3, MIDDLE)
+    project(1, 3, MIDDLE)
+    project(0, 0, FAR)
+    project(1, 0, FAR)
     ring(0, 4)
-    project(1, 3, 1, 7)
-    project(1, 0, 2, 6)
-    project(1, 1, 2, 6)
-    project(0, 0, 3, 5)
-    project(1, 0, 3, 5)
     ring(1, 4)
-    project(1, 2, 2, 6)
-    project(1, 3, 2, 6)
-    project(0, 1, 3, 5)
-    project(1, 1, 3, 5)
-    project(0, 2, 3, 5)
+    for q in range(1, 4):
+        project(0, q, FAR)
+        project(1, q, FAR)
+    add_sums(NEAR + MIDDLE + FAR)
+    for q in range(2):
+        project(0, q, LAST)
+        project(1, q, LAST)
     ring(2, 4)
-    project(1, 2, 3, 5)
-    project(0, 3, 3, 5)
-    project(1, 3, 3, 5)
-    project(0, 0, 0, 4)
     ring(3, 4)
-    project(1, 0, 0, 4)
-    for q in range(1, 4):
-        project(0, q, 0, 4)
-        project(1, q, 0, 4)
-
-    sums = []
-    for half in range(2):
-        total = jnp.zeros((8, 128), F32)
-        for zz in range(8):
-            for cc in range(2):
-                for f in range(2):
-                    total += xall[zz, cc, 2 * f + half, 512:528].astype(F32)[0:8]
-        sums.append(total[0:4] + total[4:8])
+    for q in range(2, 4):
+        project(0, q, LAST)
+        project(1, q, LAST)
+    add_sums(LAST)
+    sums = [part[0:4] + part[4:8] for part in sums]
     inverse = lax.rsqrt(jnp.concatenate(sums, axis=0) / D + 1e-05).T
     results = []
     for j in range(4):

time: 100 us -> 93.4 us (0.934)
  Pallas kernels: 100 us -> 92.6 us
    pallas_call x1, Pallas kernels: 94.6 us -> 87.2 us  [on_device(): pl.pallas_call(exchange_kernel, out_shape=jax.ShapeDtypeStruct((1024, 512...]
where the time goes in v3:
time: 93.4 us; the launch traced here: 92.6 us
  Pallas kernels  92.6 us (99%)
    pallas_call x1, Pallas kernels, on_device(): pl.pallas_call(exchange_kernel, out_shape=jax.ShapeDtypeStruct((1024, 512...  87.2 us
    pallas_call x1, Pallas kernels, on_device(): pl.pallas_call(attend_kernel, out_shape=jax.ShapeDtypeStruct((1024, 256),...  5.42 us

profile of v3, /device:TPU:1, one launch (start us, length us, event | category | flops | bytes accessed | tf_op | source)
XLA Modules:
  0.0 92.6 jit_solution(5477181452565109079)
XLA Ops:
  0.0 87.2 %exchange.1.qkv = bf16[1024,512]{1,0:T(8,128)(2,1)} custom-call(s32[2,128]{1,0:T(2,128)} %bitcast.4, s32[2,128]{1,0:T(2,128)} %bitcast.5, bf16[8,16,8,256]{3,2,1,0:T(8,128)(2,1)} %bitcast.3, bf16[256]{0:T(256)(128)(2,1)} %gain.1, bf16[128,2048]{1,0:T(8,128)(2,1)} %wkv.1, bf16[4096,256]{1,0:T(8,128)(2,1)} %wq.1), custom_call_target="tpu_custom_call" | custom-call | tf_op jit(solution)/shard_map/exchange/pallas_call | solution.py:430
  87.2 5.4 %attend.1 = bf16[1024,256]{1,0:T(8,128)(2,1)} custom-call(bf16[1024,512]{1,0:T(8,128)(2,1)} %exchange.1.qkv, s32[1,1024]{1,0:T(1,128)} %seg.1), custom_call_target="tpu_custom_call" | custom-call | tf_op jit(solution)/shard_map/attend/pallas_call | solution.py:463

commit v4 on v3

--- a/solution.py
+++ b/solution.py
@@ -31,11 +31,15 @@
     up = lax.rem(z + 1, 8) * 2 + c
     down = lax.rem(z + 7, 8) * 2 + c
 
+    def outward(k, middle):
+        return middle + lax.div(k + 1, 2) * (1 - 2 * lax.rem(k, 2))
+
     def at_offset(i):
-        return lax.rem(x + lax.div(i, 8), 4) * 8 + lax.rem(y + lax.rem(i, 8), 8)
+        dx, dy = outward(lax.div(i, 8), 2), outward(lax.rem(i, 8), 4)
+        return lax.rem(x + dx, 4) * 8 + lax.rem(y + dy, 8)
 
     def peer(i, q):
-        return lax.rem(x + lax.div(i, 2), 4) * 8 + lax.rem(lax.div(y, 4) + lax.rem(i, 2), 2) * 4 + q
+        return lax.rem(x + outward(lax.div(i, 2), 2), 4) * 8 + lax.rem(lax.div(y, 4) + lax.rem(i, 2), 2) * 4 + q
 
     def place(j):
         return lax.div(j, 8) * 2 + lax.div(lax.rem(j, 8), 4)
@@ -52,7 +56,7 @@
         pl.semaphore_signal(barrier, inc=1, device_id=(at_offset(i), t), device_id_type=MESH)
         return carry
 
-    lax.fori_loop(1, 32, greet, 0)
+    lax.fori_loop(0, 31, greet, 0)
     for who in (up, down, other):
         pl.semaphore_signal(barrier, inc=1, device_id=(l, who), device_id_type=MESH)
 
@@ -132,9 +136,9 @@
         return carry
 
     def distribute():
-        lax.fori_loop(1, 32, await_a, 0)
+        lax.fori_loop(0, 31, await_a, 0)
         lax.fori_loop(0, 32, sort, 0)
-        lax.fori_loop(1, 32, send_out, 0)
+        lax.fori_loop(0, 31, send_out, 0)
         for s in range(8):
             landed[own_q, s, own_place] = sorted_[l * 8 + s]
 
@@ -385,42 +389,46 @@
 
 
 def attend_kernel(qkv, seg, out, held, buf, take_sem, sems):
-    takes = []
-    for i in range(4):
-        at = pl.ds(256 * i, 256)
-        take = pltpu.make_async_copy(qkv.at[at], held.at[at], take_sem.at[i])
-        take.start()
-        takes.append(take)
+    take = pltpu.make_async_copy(qkv, held, take_sem)
+    take.start()
     docs = seg[...].astype(F32)
     columns = jnp.concatenate([docs[:, r * 128 : r * 128 + 128] for r in range(8)], axis=0).T
-    copies = []
+    masks = []
     for i in range(4):
         start, begin = 256 * i, max(0, 256 * i - 256)
         width = start + 256 - begin
         qdoc = jnp.concatenate([columns[:, 2 * i : 2 * i + 1], columns[:, 2 * i + 1 : 2 * i + 2]], axis=0)
         row = lax.broadcasted_iota(I32, (256, width), 0)
         col = lax.broadcasted_iota(I32, (256, width), 1)
-        allowed = (qdoc == docs[:, begin : begin + width]) & (col <= row + (start - begin))
-        takes[i].wait()
+        masks.append((qdoc == docs[:, begin : begin + width]) & (col <= row + (start - begin)))
+    take.wait()
+    scores = []
+    dims = (((1,), (1,)), ((), ()))
+    for i in range(4):
+        start, begin = 256 * i, max(0, 256 * i - 256)
+        width = start + 256 - begin
         keys = held[begin : begin + width, 2 * HD : 3 * HD]
         values = held[begin : begin + width, 3 * HD : 4 * HD]
+        both = []
         for h in range(2):
-            s = lax.dot_general(
-                held[start : start + 256, h * HD : (h + 1) * HD], keys, (((1,), (1,)), ((), ())),
-                preferred_element_type=F32,
-            )
-            masked = jnp.where(allowed, s, -1e30)
+            q = held[start : start + 256, h * HD : (h + 1) * HD]
+            s = lax.dot_general(q, keys, dims, preferred_element_type=F32)
+            both.append(s)
+        scores.append(both)
+    for i in range(4):
+        start, begin = 256 * i, max(0, 256 * i - 256)
+        width = start + 256 - begin
+        values = held[begin : begin + width, 3 * HD : 4 * HD]
+        for h in range(2):
+            masked = jnp.where(masks[i], scores[i][h], -1e30)
             top = jnp.max(masked, axis=-1, keepdims=True)
             e = jnp.exp2((masked - top) * (math.log2(math.e) / math.sqrt(HD)))
             part = jnp.dot(e.astype(BF16), values, preferred_element_type=F32)
             part = part * (1.0 / jnp.sum(e, axis=-1, keepdims=True))
             buf[start : start + 256, h * HD : (h + 1) * HD] = part.astype(BF16)
-        at = pl.ds(start, 256)
-        copy = pltpu.make_async_copy(buf.at[at], out.at[at], sems.at[i])
-        copy.start()
-        copies.append(copy)
-    for copy in copies:
-        copy.wait()
+    copy = pltpu.make_async_copy(buf, out, sems)
+    copy.start()
+    copy.wait()
 
 
 def on_device(blocks, seg_ids, dest, slot, norm_gain, w_query, w_keyval):
@@ -465,7 +473,7 @@
         out_shape=jax.ShapeDtypeStruct((1024, 256), BF16),
         in_specs=[hbm, vmem],
         out_specs=hbm,
-        scratch_shapes=[pltpu.VMEM((1024, 512), BF16), pltpu.VMEM((1024, 256), BF16), dma((4,)), dma((4,))],
+        scratch_shapes=[pltpu.VMEM((1024, 512), BF16), pltpu.VMEM((1024, 256), BF16), dma, dma],
         compiler_params=pltpu.CompilerParams(vmem_limit_bytes=60 * 1024 * 1024),
         name="attend",
     )(qkv, seg_ids)

time: 93.4 us -> 92 us (0.985)
  Pallas kernels: 92.6 us -> 90.8 us
    pallas_call x1, Pallas kernels: 5.42 us -> 4.35 us  [on_device(): pl.pallas_call(attend_kernel, out_shape=jax.ShapeDtypeStruct((1024, 256),...]
where the time goes in v4:
time: 92 us; the launch traced here: 90.8 us
  Pallas kernels  90.8 us (99%)
    pallas_call x1, Pallas kernels, on_device(): pl.pallas_call(exchange_kernel, out_shape=jax.ShapeDtypeStruct((1024, 512...  86.4 us
    pallas_call x1, Pallas kernels, on_device(): pl.pallas_call(attend_kernel, out_shape=jax.ShapeDtypeStruct((1024, 256),...  4.35 us

profile of v4, /device:TPU:1, one launch (start us, length us, event | category | flops | bytes accessed | tf_op | source)
XLA Modules:
  0.0 90.8 jit_solution(5312490620378037870)
XLA Ops:
  0.0 86.4 %exchange.1.qkv = bf16[1024,512]{1,0:T(8,128)(2,1)} custom-call(s32[2,128]{1,0:T(2,128)} %bitcast.4, s32[2,128]{1,0:T(2,128)} %bitcast.5, bf16[8,16,8,256]{3,2,1,0:T(8,128)(2,1)} %bitcast.3, bf16[256]{0:T(256)(128)(2,1)} %gain.1, bf16[128,2048]{1,0:T(8,128)(2,1)} %wkv.1, bf16[4096,256]{1,0:T(8,128)(2,1)} %wq.1), custom_call_target="tpu_custom_call" | custom-call | tf_op jit(solution)/shard_map/exchange/pallas_call | solution.py:438
  86.4 4.3 %attend.1 = bf16[1024,256]{1,0:T(8,128)(2,1)} custom-call(bf16[1024,512]{1,0:T(8,128)(2,1)} %exchange.1.qkv, s32[1,1024]{1,0:T(1,128)} %seg.1), custom_call_target="tpu_custom_call" | custom-call | tf_op jit(solution)/shard_map/attend/pallas_call | solution.py:471

commit v5 on v4

--- a/solution.py
+++ b/solution.py
@@ -209,6 +209,11 @@
 
     row = lax.broadcasted_iota(I32, (8, 128), 0)
 
+    squares = {}
+
+    def part(zo, cc, q):
+        return xall.at[zo, cc, q, pl.ds(0, 512 if q < 2 else ROWS)]
+
     def arrive(q):
         def await_b(i, carry):
             j = peer(i, q)
@@ -236,15 +241,19 @@
             return jnp.where(lax.rem(row, 4) == j, sums, total)
 
         total = lax.fori_loop(0, 4, scale, jnp.zeros((8, 128), F32))
+        if f == 0:
+            squares[q] = total
+            return
+        total = total + squares[q - 2]
         hi = total.astype(BF16).astype(F32)
         tile = jnp.where(row < 4, hi, total - hi)
         xall[z, c, q, 512:528] = jnp.concatenate([tile, jnp.zeros((8, 128), F32)], axis=0).astype(BF16)
 
     def to_ring(zo, q, way, step):
         pltpu.make_async_remote_copy(
-            src_ref=xall.at[zo, c, q],
-            dst_ref=xall.at[zo, c, q],
-            send_sem=send_z,
+            src_ref=part(zo, c, q),
+            dst_ref=part(zo, c, q),
+            send_sem=send_z.at[q // 2],
             recv_sem=recv_z.at[q, way, step],
             device_id=(l, up if way == 0 else down),
             device_id_type=MESH,
@@ -252,9 +261,9 @@
 
     def to_sibling(zo, q, k):
         pltpu.make_async_remote_copy(
-            src_ref=xall.at[zo, c, q],
-            dst_ref=xall.at[zo, c, q],
-            send_sem=send_d,
+            src_ref=part(zo, c, q),
+            dst_ref=part(zo, c, q),
+            send_sem=send_d.at[q // 2],
             recv_sem=recv_d.at[q, k],
             device_id=(l, other),
             device_id_type=MESH,
@@ -271,7 +280,7 @@
                 continue
             k = (8 - step) if way == 0 else step
             zo = lax.rem(z + k, 8)
-            pending(xall.at[zo, c, q], recv_z.at[q, way, step - 1]).wait()
+            pending(part(zo, c, q), recv_z.at[q, way, step - 1]).wait()
             if step < 3 or (step == 3 and way == q % 2):
                 to_ring(zo, q, way, step)
             to_sibling(zo, q, k)
@@ -281,7 +290,7 @@
         zs = [lax.rem(z + k, 8) for k in group]
         if kind == 0:
             for k, zo in zip(group, zs):
-                pending(xall.at[zo, 1 - c, q], recv_d.at[q, k]).wait()
+                pending(part(zo, 1 - c, q), recv_d.at[q, k]).wait()
 
         pairs = [(zo, cc) for zo in zs for cc in range(2)]
         lhs = jnp.concatenate([xall[zo, cc, q, 0:512] for zo, cc in pairs], axis=1)
@@ -301,8 +310,7 @@
             total = jnp.zeros((8, 128), F32)
             for k in ks:
                 for cc in range(2):
-                    for f in range(2):
-                        total += xall[lax.rem(z + k, 8), cc, 2 * f + half, 512:528].astype(F32)[0:8]
+                    total += xall[lax.rem(z + k, 8), cc, 2 + half, 512:528].astype(F32)[0:8]
             sums[half] = total if sums[half] is None else sums[half] + total
 
     NEAR, MIDDLE, FAR, LAST = (0, 1, 7), (2, 6), (3, 5), (4,)
@@ -379,8 +387,10 @@
 
     pending(gathered.at[pl.ds(0, 248)], send_a).wait()
     pending(gathered.at[pl.ds(0, 248)], send_b).wait()
-    pending(xall.at[pl.ds(0, 7), 0], send_z).wait()
-    pending(xall.at[:, 0], send_d).wait()
+    for f, rows in enumerate((512, ROWS)):
+        chunks = pl.ds(2 * f, 2)
+        pending(xall.at[pl.ds(0, 7), 0, chunks, pl.ds(0, rows)], send_z.at[f]).wait()
+        pending(xall.at[:, 0, chunks, pl.ds(0, rows)], send_d.at[f]).wait()
     pending(wk.at[pl.ds(0, 7), half_rows], send_w.at[0]).wait()
     pending(wk.at[pl.ds(0, 24), half_rows], send_w.at[1]).wait()
     pending(wk.at[:, half_rows], send_w.at[2]).wait()
@@ -453,7 +463,7 @@
             pltpu.VMEM((1, 256), I32),
             pltpu.SMEM((1, 256), I32),
             dma, dma, dma, dma((4,)), dma,
-            dma, dma((32,)), dma, dma((32,)), dma, dma((4, 2, 4)), dma, dma((4, 8)),
+            dma, dma((32,)), dma, dma((32,)), dma((2,)), dma((4, 2, 4)), dma((2,)), dma((4, 8)),
             dma((3,)), dma((8,)), dma((2, 2)), dma,
         ],
         compiler_params=pltpu.CompilerParams(

time: 92 us -> 91.3 us (level)
  no operation moved by 1% of the time
where the time goes in v5:
time: 91.3 us; the launch traced here: 90.4 us
  Pallas kernels  90.4 us (99%)
    pallas_call x1, Pallas kernels, on_device(): pl.pallas_call(exchange_kernel, out_shape=jax.ShapeDtypeStruct((1024, 512...  86 us
    pallas_call x1, Pallas kernels, on_device(): pl.pallas_call(attend_kernel, out_shape=jax.ShapeDtypeStruct((1024, 256),...  4.34 us

profile of v5, /device:TPU:1, one launch (start us, length us, event | category | flops | bytes accessed | tf_op | source)
XLA Modules:
  0.0 90.4 jit_solution(9311744065649564933)
XLA Ops:
  0.0 86.0 %exchange.1.qkv = bf16[1024,512]{1,0:T(8,128)(2,1)} custom-call(s32[2,128]{1,0:T(2,128)} %bitcast.4, s32[2,128]{1,0:T(2,128)} %bitcast.5, bf16[8,16,8,256]{3,2,1,0:T(8,128)(2,1)} %bitcast.3, bf16[256]{0:T(256)(128)(2,1)} %gain.1, bf16[128,2048]{1,0:T(8,128)(2,1)} %wkv.1, bf16[4096,256]{1,0:T(8,128)(2,1)} %wq.1), custom_call_target="tpu_custom_call" | custom-call | tf_op jit(solution)/shard_map/exchange/pallas_call | solution.py:448
  86.0 4.3 %attend.1 = bf16[1024,256]{1,0:T(8,128)(2,1)} custom-call(bf16[1024,512]{1,0:T(8,128)(2,1)} %exchange.1.qkv, s32[1,1024]{1,0:T(1,128)} %seg.1), custom_call_target="tpu_custom_call" | custom-call | tf_op jit(solution)/shard_map/attend/pallas_call | solution.py:481
